TPU v7x, 32 devices: a whole 2x2x4 slice. The times are simulated.
32 devices in a mesh: tm: 4 (over x, core), anta: 4 (over z), antb: 2 (over y).
Axes of the slice: x: 2, y: 2, z: 4, core: 2. Of those that a mesh axis runs over, the one named last changes fastest.
Arguments:
- samples: bfloat16 [2, 512, 6144], P('antb', 'anta', 'tm'), may hold values from -6 to 6
Outputs:
- correlation: float32 [256, 2, 512, 2, 512], P('tm', None, 'anta', 'antb')
All inputs are finite; a program needn't handle non-finite values.
Results may differ from a plain program's by a relative error of at most 0.0003.
Values may be sent and summed in bfloat16 or wider, within the bound.
A program may use at most 128 MiB of HBM per device.

v0:
```python
import math
import jax
import jax.numpy as jnp
from jax import lax
from jax.sharding import PartitionSpec as P

ANTENNA_COUNT = 512
POLARISATION_NUM = 2
LAG_TOTAL = 256


def lag_terms(row_padded, columns, lag_start, lag_count, window_len):
    group_len = math.gcd(lag_count, 8)
    flat_cols = columns.reshape(columns.shape[1], columns.shape[2])

    def one_group(group_index):
        first_lag = lag_start + group_index * group_len
        pieces = [
            lax.dynamic_slice_in_dim(row_padded, LAG_TOTAL - first_lag - step_index, window_len, 1)
            for step_index in range(group_len)
        ]
        stacked = jnp.stack(pieces, 0)
        return jnp.einsum("kit,jt->kij", stacked, flat_cols, preferred_element_type=jnp.float32)

    grouped = lax.map(one_group, jnp.arange(lag_count // group_len, dtype=jnp.int32))
    return grouped.reshape(lag_count, row_padded.shape[0], flat_cols.shape[0])


def collect_rows(own_window):
    return lax.all_gather(own_window, "antb", axis=0, tiled=True)


def per_device(samples):
    antenna_total = samples.shape[1]
    block_len = samples.shape[2]
    tm_size = lax.axis_size("tm")
    lag_portion = LAG_TOTAL // tm_size
    full_length = block_len * tm_size
    factor = 1.0 / math.sqrt(full_length)
    lag_start = lax.axis_index("tm") * lag_portion
    col_tiles = lax.all_gather(samples, "anta", axis=1, tiled=True)
    columns = lax.all_gather(col_tiles, "tm", axis=2, tiled=True)
    own_rows = lax.dynamic_slice_in_dim(
        columns, lax.axis_index("anta") * antenna_total, antenna_total, 1
    )
    row_samples = collect_rows(own_rows)
    row_padded = jnp.pad(
        row_samples.reshape(POLARISATION_NUM * antenna_total, full_length), ((0, 0), (LAG_TOTAL, 0))
    )
    lag_group_block = lag_terms(row_padded, columns, lag_start, lag_portion, full_length)
    accumulated_sum = lag_group_block.reshape(
        lag_portion, POLARISATION_NUM, antenna_total, 1, ANTENNA_COUNT
    )
    return accumulated_sum * factor


def solution(mesh):
    return jax.shard_map(
        per_device,
        mesh=mesh,
        in_specs=(P("antb", "anta", "tm"),),
        out_specs=P("tm", None, "anta", "antb", None),
        check_vma=False,
    )
```

profile of v0, /device:TPU:0, one launch (start us, length us, event | category | flops | bytes accessed | tf_op | source)
XLA Modules:
  0.0 584.9 jit_solution(11511170079034413192)
XLA Ops:
  7.3 41.4 %all-gather.4.cloned.1.call-done = bf16[1,512,1536]{2,1,0:T(8,128)(2,1)} async-done(((bf16[1,128,1536]{2,1,0:T(8,128)(2,1)}), bf16[1,512,1536]{2,1,0:T(8,128)(2,1)}) %all-gather.4.cloned.1.call-update) | async-done | bytes 1572880 | tf_op jit(solution)/shard_map/all_gather | solution.py:41
  48.8 46.7 %all-gather.6.cloned.1.call-done = bf16[1,512,6144]{2,1,0:T(8,128)(2,1)} async-done(((bf16[1,512,1536]{2,1,0:T(8,128)(2,1)}), bf16[1,512,6144]{2,1,0:T(8,128)(2,1)}) %all-gather.6.cloned.1.call-update) | async-done | bytes 6291472 | tf_op jit(solution)/shard_map/all_gather | solution.py:42
  98.2 45.1 %all-gather.8.cloned.1.call-done = bf16[2,128,6144]{2,1,0:T(8,128)(2,1)} async-done(((bf16[1,128,6144]{2,1,0:T(8,128)(2,1)}), bf16[2,128,6144]{2,1,0:T(8,128)(2,1)}) %all-gather.8.cloned.1.call-update) | async-done | bytes 3145744 | tf_op jit(solution)/shard_map/all_gather | solution.py:30
  145.4 360.6 %while.14 = (s32[]{:T(128)}, f32[8,8,256,512]{3,2,1,0:T(8,128)}, s32[8]{0:T(128)S(1)}, s32[]{:T(128)}, bf16[256,6400]{1,0:T(8,128)(2,1)S(1)}, /*index=5*/bf16[51...) while((s32[]{:T(128)}, f32[8,8,256,512]{3,2,1,0:T(8,128)}, ...), condition=%wide.region_1.2_spmd, body=%wide.region_0.1_spmd.sunk | while | flops 12884901888 | bytes 85984392 | solution.py:25
  146.7 2.8 bitcast_dynamic-update-slice_fusion.18
  149.5 2.9 bitcast_dynamic-update-slice_fusion.19
  152.4 2.9 bitcast_dynamic-update-slice_fusion.20
  160.9 2.8 bitcast_dynamic-update-slice_fusion.23
  166.6 2.8 bitcast_dynamic-update-slice_fusion.25
  169.4 21.0 %bitcast_dynamic-update-slice_fusion.26 = f32[8,8,256,512]{3,2,1,0:T(8,128)} fusion(f32[8,8,256,512]{3,2,1,0:T(8,128)} %get-tuple-element.216, s32[]{:T(128)} %get-tuple-element.215, bf16[8,256,6144]{2,1,0:T(8,128)(2,1)} %bitcast_dynamic-update-slice_fusion.25, bf16[512,6144]{1,0:T(8,128)(2,1)} %get-tuple-element.245), kind=kOutput, calls=%fused_computation.2.clone.1 | convolution fusion | flops 12884901888 | bytes 35652096 | tf_op jit(solution)/shard_map/while/body/eval_jaxpr/kit,jt->kij/dot_general | solution.py:23
  191.8 2.8 bitcast_dynamic-update-slice_fusion.18
  194.6 2.9 bitcast_dynamic-update-slice_fusion.19
  197.5 2.9 bitcast_dynamic-update-slice_fusion.20
  206.0 2.8 bitcast_dynamic-update-slice_fusion.23
  211.7 2.8 bitcast_dynamic-update-slice_fusion.25
  214.5 21.1 %bitcast_dynamic-update-slice_fusion.26 = f32[8,8,256,512]{3,2,1,0:T(8,128)} fusion(f32[8,8,256,512]{3,2,1,0:T(8,128)} %get-tuple-element.216, s32[]{:T(128)} %get-tuple-element.215, bf16[8,256,6144]{2,1,0:T(8,128)(2,1)} %bitcast_dynamic-update-slice_fusion.25, bf16[512,6144]{1,0:T(8,128)(2,1)} %get-tuple-element.245), kind=kOutput, calls=%fused_computation.2.clone.1 | convolution fusion | flops 12884901888 | bytes 35652096 | tf_op jit(solution)/shard_map/while/body/eval_jaxpr/kit,jt->kij/dot_general | solution.py:23
  236.8 2.8 bitcast_dynamic-update-slice_fusion.18
  239.7 2.9 bitcast_dynamic-update-slice_fusion.19
  242.6 2.9 bitcast_dynamic-update-slice_fusion.20
  251.1 2.8 bitcast_dynamic-update-slice_fusion.23
  259.6 21.1 %bitcast_dynamic-update-slice_fusion.26 = f32[8,8,256,512]{3,2,1,0:T(8,128)} fusion(f32[8,8,256,512]{3,2,1,0:T(8,128)} %get-tuple-element.216, s32[]{:T(128)} %get-tuple-element.215, bf16[8,256,6144]{2,1,0:T(8,128)(2,1)} %bitcast_dynamic-update-slice_fusion.25, bf16[512,6144]{1,0:T(8,128)(2,1)} %get-tuple-element.245), kind=kOutput, calls=%fused_computation.2.clone.1 | convolution fusion | flops 12884901888 | bytes 35652096 | tf_op jit(solution)/shard_map/while/body/eval_jaxpr/kit,jt->kij/dot_general | solution.py:23
  281.9 2.8 bitcast_dynamic-update-slice_fusion.18
  284.8 2.9 bitcast_dynamic-update-slice_fusion.19
  287.6 2.9 bitcast_dynamic-update-slice_fusion.20
  296.2 2.8 bitcast_dynamic-update-slice_fusion.23
  304.7 21.1 %bitcast_dynamic-update-slice_fusion.26 = f32[8,8,256,512]{3,2,1,0:T(8,128)} fusion(f32[8,8,256,512]{3,2,1,0:T(8,128)} %get-tuple-element.216, s32[]{:T(128)} %get-tuple-element.215, bf16[8,256,6144]{2,1,0:T(8,128)(2,1)} %bitcast_dynamic-update-slice_fusion.25, bf16[512,6144]{1,0:T(8,128)(2,1)} %get-tuple-element.245), kind=kOutput, calls=%fused_computation.2.clone.1 | convolution fusion | flops 12884901888 | bytes 35652096 | tf_op jit(solution)/shard_map/while/body/eval_jaxpr/kit,jt->kij/dot_general | solution.py:23
  327.0 2.8 bitcast_dynamic-update-slice_fusion.18
  329.8 2.9 bitcast_dynamic-update-slice_fusion.19
  332.7 2.9 bitcast_dynamic-update-slice_fusion.20
  346.9 2.8 bitcast_dynamic-update-slice_fusion.25
  349.7 21.1 %bitcast_dynamic-update-slice_fusion.26 = f32[8,8,256,512]{3,2,1,0:T(8,128)} fusion(f32[8,8,256,512]{3,2,1,0:T(8,128)} %get-tuple-element.216, s32[]{:T(128)} %get-tuple-element.215, bf16[8,256,6144]{2,1,0:T(8,128)(2,1)} %bitcast_dynamic-update-slice_fusion.25, bf16[512,6144]{1,0:T(8,128)(2,1)} %get-tuple-element.245), kind=kOutput, calls=%fused_computation.2.clone.1 | convolution fusion | flops 12884901888 | bytes 35652096 | tf_op jit(solution)/shard_map/while/body/eval_jaxpr/kit,jt->kij/dot_general | solution.py:23
  372.1 2.8 bitcast_dynamic-update-slice_fusion.18
  374.9 2.9 bitcast_dynamic-update-slice_fusion.19
  377.8 2.9 bitcast_dynamic-update-slice_fusion.20
  392.0 2.8 bitcast_dynamic-update-slice_fusion.25
  394.8 21.1 %bitcast_dynamic-update-slice_fusion.26 = f32[8,8,256,512]{3,2,1,0:T(8,128)} fusion(f32[8,8,256,512]{3,2,1,0:T(8,128)} %get-tuple-element.216, s32[]{:T(128)} %get-tuple-element.215, bf16[8,256,6144]{2,1,0:T(8,128)(2,1)} %bitcast_dynamic-update-slice_fusion.25, bf16[512,6144]{1,0:T(8,128)(2,1)} %get-tuple-element.245), kind=kOutput, calls=%fused_computation.2.clone.1 | convolution fusion | flops 12884901888 | bytes 35652096 | tf_op jit(solution)/shard_map/while/body/eval_jaxpr/kit,jt->kij/dot_general | solution.py:23
  417.2 2.8 bitcast_dynamic-update-slice_fusion.18
  420.0 2.9 bitcast_dynamic-update-slice_fusion.19
  422.9 2.9 bitcast_dynamic-update-slice_fusion.20
  431.4 2.8 bitcast_dynamic-update-slice_fusion.23
  439.9 21.1 %bitcast_dynamic-update-slice_fusion.26 = f32[8,8,256,512]{3,2,1,0:T(8,128)} fusion(f32[8,8,256,512]{3,2,1,0:T(8,128)} %get-tuple-element.216, s32[]{:T(128)} %get-tuple-element.215, bf16[8,256,6144]{2,1,0:T(8,128)(2,1)} %bitcast_dynamic-update-slice_fusion.25, bf16[512,6144]{1,0:T(8,128)(2,1)} %get-tuple-element.245), kind=kOutput, calls=%fused_computation.2.clone.1 | convolution fusion | flops 12884901888 | bytes 35652096 | tf_op jit(solution)/shard_map/while/body/eval_jaxpr/kit,jt->kij/dot_general | solution.py:23
  462.2 2.8 bitcast_dynamic-update-slice_fusion.18
  465.1 2.9 bitcast_dynamic-update-slice_fusion.19
  467.9 2.9 bitcast_dynamic-update-slice_fusion.20
  476.5 2.8 bitcast_dynamic-update-slice_fusion.23
  485.0 21.1 %bitcast_dynamic-update-slice_fusion.26 = f32[8,8,256,512]{3,2,1,0:T(8,128)} fusion(f32[8,8,256,512]{3,2,1,0:T(8,128)} %get-tuple-element.216, s32[]{:T(128)} %get-tuple-element.215, bf16[8,256,6144]{2,1,0:T(8,128)(2,1)} %bitcast_dynamic-update-slice_fusion.25, bf16[512,6144]{1,0:T(8,128)(2,1)} %get-tuple-element.245), kind=kOutput, calls=%fused_computation.2.clone.1 | convolution fusion | flops 12884901888 | bytes 35652096 | tf_op jit(solution)/shard_map/while/body/eval_jaxpr/kit,jt->kij/dot_general | solution.py:23
  506.0 23.9 %broadcast_multiply_fusion = f32[8,8,256,512]{3,2,1,0:T(8,128)} fusion(f32[8,8,256,512]{3,2,1,0:T(8,128)} %get-tuple-element.140), kind=kLoop, calls=%fused_computation.11 | loop fusion | flops 8388608 | bytes 67108864 | tf_op jit(solution)/shard_map/mul | solution.py:54
  530.0 48.4 %mul.39 = f32[64,2,128,1,512]{4,3,2,1,0:T(1,128)} reshape(f32[8,8,256,512]{3,2,1,0:T(8,128)} %broadcast_multiply_fusion) | data formatting | bytes 67108864 | tf_op jit(solution)/shard_map/mul | solution.py:54
  (48 shorter events, 95.5 us)
Async XLA Ops:
  6.5 42.1 %all-gather.4.cloned.1.call-start = ((), (), s32[]{:S(2)}) async-start(), calls=%async_computation | async-start | bytes 1966080 | tf_op jit(solution)/shard_map/all_gather | solution.py:41
  7.3 88.2 %all-gather.6.cloned.1.call-start = ((), (), s32[]{:S(2)}) async-start(), calls=%async_computation.1 | async-start | bytes 7864320 | tf_op jit(solution)/shard_map/all_gather | solution.py:42
  48.7 94.6 %all-gather.8.cloned.1.call-start = ((), (), s32[]{:S(2)}) async-start(), calls=%async_computation.2 | async-start | bytes 4718592 | tf_op jit(solution)/shard_map/all_gather | solution.py:30
Sparse Core Ops, SparseCore 0:
  8.9 39.7 all-gather.3
  50.2 45.2 all-gather.5
  98.3 44.9 all-gather.7
where the time goes:
time: 586 us; the launch traced here: 585 us
  local copies, waits for them, and re-layouts  240 us (41%)
  matrix products  168 us (29%)
  waiting for transfers between devices  134 us (23%)
  other arithmetic  23.9 us (4%)
  between operations  13.1 us (2%)
    dot_general x8, matrix products, one_group(): jnp.einsum('kit,jt->kij', stacked, flat_cols, preferred_element_type=jnp....  168 us
    while x56, local copies, waits for them, and re-layouts  159 us
    mul x1, local copies, waits for them, and re-layouts, per_device(): return accumulated_sum * factor  48.4 us
    all_gather x1, waiting for transfers between devices, per_device(): columns = lax.all_gather(col_tiles, 'tm', axis=2, tiled=True)  46.7 us
    all_gather x1, waiting for transfers between devices, collect_rows(): return lax.all_gather(own_window, 'antb', axis=0, tiled=True)  45.1 us
    all_gather x1, waiting for transfers between devices, per_device(): col_tiles = lax.all_gather(samples, 'anta', axis=1, tiled=True)  41.4 us
    mul x1, other arithmetic, per_device(): return accumulated_sum * factor  23.9 us
    another operation x8, local copies, waits for them, and re-layouts, one_group(): stacked = jnp.stack(pieces, 0)  22.7 us
  transfers between devices with their start and end apart: 3, of which 3 were waited for; matrix products, arithmetic and copies ran while one was open for 0% of the time, Pallas kernels for 0%

commit v1 on v0

--- a/solution.py
+++ b/solution.py
@@ -39,7 +39,9 @@
     factor = 1.0 / math.sqrt(full_length)
     lag_start = lax.axis_index("tm") * lag_portion
     col_tiles = lax.all_gather(samples, "anta", axis=1, tiled=True)
-    columns = lax.all_gather(col_tiles, "tm", axis=2, tiled=True)
+    columns = jnp.concatenate(
+        lax.all_to_all(jnp.stack([col_tiles] * lax.axis_size("tm")), "tm", 0, 0), axis=2
+    )
     own_rows = lax.dynamic_slice_in_dim(
         columns, lax.axis_index("anta") * antenna_total, antenna_total, 1
     )

time: 586 us -> 629 us (1.073)
  local copies, waits for them, and re-layouts: 240 us -> 263 us
  waiting for transfers between devices: 134 us -> 147 us
    all_to_all x0 -> x1, waiting for transfers between devices: none -> 70.6 us  [per_device(): lax.all_to_all(jnp.stack([col_tiles] * lax.axis_size('tm')), 'tm', 0, 0)]
    all_gather x1 -> x0, waiting for transfers between devices: 46.7 us -> none  [per_device(): columns = lax.all_gather(col_tiles, 'tm', axis=2, tiled=True)]
    all_gather x1, waiting for transfers between devices: 45.1 us -> 34.2 us  [collect_rows(): return lax.all_gather(own_window, 'antb', axis=0, tiled=True)]
    while x56 -> x57, local copies, waits for them, and re-layouts: 159 us -> 168 us
    all_to_all x0 -> x1, local copies, waits for them, and re-layouts: none -> 8.65 us  [per_device(): lax.all_to_all(jnp.stack([col_tiles] * lax.axis_size('tm')), 'tm', 0, 0)]
  transfers between devices with their start and end apart: 3 -> 3, of which waited for: 3 -> 3; matrix products, arithmetic and copies ran while one was open for 0% -> 1% of each run, Pallas kernels for 0% -> 0%
where the time goes in v1:
time: 629 us; the launch traced here: 627 us
  local copies, waits for them, and re-layouts  263 us (42%)
  matrix products  168 us (27%)
  waiting for transfers between devices  147 us (23%)
  other arithmetic  23.9 us (4%)
  between operations  13.4 us (2%)
    dot_general x8, matrix products, one_group(): jnp.einsum('kit,jt->kij', stacked, flat_cols, preferred_element_type=jnp....  168 us
    while x56, local copies, waits for them, and re-layouts  159 us
    all_to_all x1, waiting for transfers between devices, per_device(): lax.all_to_all(jnp.stack([col_tiles] * lax.axis_size('tm')), 'tm', 0, 0)  70.6 us
    mul x1, local copies, waits for them, and re-layouts, per_device(): return accumulated_sum * factor  48.4 us
    all_gather x1, waiting for transfers between devices, per_device(): col_tiles = lax.all_gather(samples, 'anta', axis=1, tiled=True)  41.4 us
    all_gather x1, waiting for transfers between devices, collect_rows(): return lax.all_gather(own_window, 'antb', axis=0, tiled=True)  34.2 us
    mul x1, other arithmetic, per_device(): return accumulated_sum * factor  23.9 us
    another operation x8, local copies, waits for them, and re-layouts, one_group(): stacked = jnp.stack(pieces, 0)  22.7 us
  transfers between devices with their start and end apart: 3, of which 3 were waited for; matrix products, arithmetic and copies ran while one was open for 1% of the time, Pallas kernels for 0%

profile of v1, /device:TPU:0, one launch (start us, length us, event | category | flops | bytes accessed | tf_op | source)
XLA Modules:
  0.0 626.6 jit_solution(14686554505640058495)
XLA Ops:
  7.3 41.4 %all-gather.3.cloned.1.call-done = bf16[1,512,1536]{2,1,0:T(8,128)(2,1)} async-done(((bf16[1,128,1536]{2,1,0:T(8,128)(2,1)}), bf16[1,512,1536]{2,1,0:T(8,128)(2,1)}) %all-gather.3.cloned.1.call-update) | async-done | bytes 1572880 | tf_op jit(solution)/shard_map/all_gather | solution.py:41
  48.7 4.6 stack.88
  53.3 5.2 all-to-all-start
  58.6 70.6 %all-to-all-done = bf16[4,1,512,1536]{3,2,1,0:T(8,128)(2,1)} async-done(((bf16[4,1,512,1536]{3,2,1,0:T(8,128)(2,1)}), bf16[4,1,512,1536]{3,2,1,0:T(8,128)(2,1)}, u32[]{:S(2)}, u32[]{:S(2)}) %all-to-all-start) | async-done | bytes 6291488 | tf_op jit(solution)/shard_map/all_to_all | solution.py:43
  129.2 8.7 %copy.2 = bf16[4,1,512,1536]{2,3,0,1:T(8,128)(2,1)} copy(bf16[4,1,512,1536]{3,2,1,0:T(8,128)(2,1)} %all-to-all-done) | data formatting | bytes 12582912 | tf_op jit(solution)/shard_map/all_to_all | solution.py:43
  141.0 8.8 %copy.4 = bf16[512,6144]{1,0:T(8,128)(2,1)} copy(bf16[512,6144]{0,1:T(8,128)(2,1)} %bitcast.59) | data formatting | bytes 12582912 | tf_op jit(solution)/shard_map/while | solution.py:25
  149.7 34.2 %all-gather.5.cloned.1.call-done = bf16[2,128,6144]{2,1,0:T(8,128)(2,1)} async-done(((bf16[1,128,6144]{2,1,0:T(8,128)(2,1)}), bf16[2,128,6144]{2,1,0:T(8,128)(2,1)}) %all-gather.5.cloned.1.call-update) | async-done | bytes 3145744 | tf_op jit(solution)/shard_map/all_gather | solution.py:30
  186.1 361.4 %while.14 = (s32[]{:T(128)}, f32[8,8,256,512]{3,2,1,0:T(8,128)}, s32[8]{0:T(128)S(1)}, s32[]{:T(128)}, bf16[256,6400]{1,0:T(8,128)(2,1)S(1)}, /*index=5*/bf16[51...) while((s32[]{:T(128)}, f32[8,8,256,512]{3,2,1,0:T(8,128)}, ...), condition=%wide.region_1.2_spmd, body=%wide.region_0.1_spmd.sunk | while | flops 12884901888 | bytes 85984392 | solution.py:25
  187.5 2.9 bitcast_dynamic-update-slice_fusion.18
  190.3 2.9 bitcast_dynamic-update-slice_fusion.19
  193.2 2.9 bitcast_dynamic-update-slice_fusion.20
  201.7 2.8 bitcast_dynamic-update-slice_fusion.23
  207.4 2.8 bitcast_dynamic-update-slice_fusion.25
  210.2 21.1 %bitcast_dynamic-update-slice_fusion.26 = f32[8,8,256,512]{3,2,1,0:T(8,128)} fusion(f32[8,8,256,512]{3,2,1,0:T(8,128)} %get-tuple-element.222, s32[]{:T(128)} %get-tuple-element.221, bf16[8,256,6144]{2,1,0:T(8,128)(2,1)} %bitcast_dynamic-update-slice_fusion.25, bf16[512,6144]{1,0:T(8,128)(2,1)} %get-tuple-element.251), kind=kOutput, calls=%fused_computation.2.clone.1 | convolution fusion | flops 12884901888 | bytes 35652096 | tf_op jit(solution)/shard_map/while/body/eval_jaxpr/kit,jt->kij/dot_general | solution.py:23
  232.6 2.9 bitcast_dynamic-update-slice_fusion.18
  235.5 2.9 bitcast_dynamic-update-slice_fusion.19
  238.4 2.9 bitcast_dynamic-update-slice_fusion.20
  246.9 2.8 bitcast_dynamic-update-slice_fusion.23
  252.6 2.8 bitcast_dynamic-update-slice_fusion.25
  255.4 21.1 %bitcast_dynamic-update-slice_fusion.26 = f32[8,8,256,512]{3,2,1,0:T(8,128)} fusion(f32[8,8,256,512]{3,2,1,0:T(8,128)} %get-tuple-element.222, s32[]{:T(128)} %get-tuple-element.221, bf16[8,256,6144]{2,1,0:T(8,128)(2,1)} %bitcast_dynamic-update-slice_fusion.25, bf16[512,6144]{1,0:T(8,128)(2,1)} %get-tuple-element.251), kind=kOutput, calls=%fused_computation.2.clone.1 | convolution fusion | flops 12884901888 | bytes 35652096 | tf_op jit(solution)/shard_map/while/body/eval_jaxpr/kit,jt->kij/dot_general | solution.py:23
  277.8 2.9 bitcast_dynamic-update-slice_fusion.18
  280.7 2.9 bitcast_dynamic-update-slice_fusion.19
  283.5 2.9 bitcast_dynamic-update-slice_fusion.20
  292.0 2.8 bitcast_dynamic-update-slice_fusion.23
  297.7 2.8 bitcast_dynamic-update-slice_fusion.25
  300.6 21.1 %bitcast_dynamic-update-slice_fusion.26 = f32[8,8,256,512]{3,2,1,0:T(8,128)} fusion(f32[8,8,256,512]{3,2,1,0:T(8,128)} %get-tuple-element.222, s32[]{:T(128)} %get-tuple-element.221, bf16[8,256,6144]{2,1,0:T(8,128)(2,1)} %bitcast_dynamic-update-slice_fusion.25, bf16[512,6144]{1,0:T(8,128)(2,1)} %get-tuple-element.251), kind=kOutput, calls=%fused_computation.2.clone.1 | convolution fusion | flops 12884901888 | bytes 35652096 | tf_op jit(solution)/shard_map/while/body/eval_jaxpr/kit,jt->kij/dot_general | solution.py:23
  323.0 2.9 bitcast_dynamic-update-slice_fusion.18
  325.8 2.9 bitcast_dynamic-update-slice_fusion.19
  328.7 2.9 bitcast_dynamic-update-slice_fusion.20
  345.7 21.1 %bitcast_dynamic-update-slice_fusion.26 = f32[8,8,256,512]{3,2,1,0:T(8,128)} fusion(f32[8,8,256,512]{3,2,1,0:T(8,128)} %get-tuple-element.222, s32[]{:T(128)} %get-tuple-element.221, bf16[8,256,6144]{2,1,0:T(8,128)(2,1)} %bitcast_dynamic-update-slice_fusion.25, bf16[512,6144]{1,0:T(8,128)(2,1)} %get-tuple-element.251), kind=kOutput, calls=%fused_computation.2.clone.1 | convolution fusion | flops 12884901888 | bytes 35652096 | tf_op jit(solution)/shard_map/while/body/eval_jaxpr/kit,jt->kij/dot_general | solution.py:23
  368.1 2.9 bitcast_dynamic-update-slice_fusion.18
  371.0 2.9 bitcast_dynamic-update-slice_fusion.19
  373.9 2.9 bitcast_dynamic-update-slice_fusion.20
  390.9 21.1 %bitcast_dynamic-update-slice_fusion.26 = f32[8,8,256,512]{3,2,1,0:T(8,128)} fusion(f32[8,8,256,512]{3,2,1,0:T(8,128)} %get-tuple-element.222, s32[]{:T(128)} %get-tuple-element.221, bf16[8,256,6144]{2,1,0:T(8,128)(2,1)} %bitcast_dynamic-update-slice_fusion.25, bf16[512,6144]{1,0:T(8,128)(2,1)} %get-tuple-element.251), kind=kOutput, calls=%fused_computation.2.clone.1 | convolution fusion | flops 12884901888 | bytes 35652096 | tf_op jit(solution)/shard_map/while/body/eval_jaxpr/kit,jt->kij/dot_general | solution.py:23
  413.3 2.9 bitcast_dynamic-update-slice_fusion.18
  416.2 2.9 bitcast_dynamic-update-slice_fusion.19
  419.0 2.9 bitcast_dynamic-update-slice_fusion.20
  436.1 21.1 %bitcast_dynamic-update-slice_fusion.26 = f32[8,8,256,512]{3,2,1,0:T(8,128)} fusion(f32[8,8,256,512]{3,2,1,0:T(8,128)} %get-tuple-element.222, s32[]{:T(128)} %get-tuple-element.221, bf16[8,256,6144]{2,1,0:T(8,128)(2,1)} %bitcast_dynamic-update-slice_fusion.25, bf16[512,6144]{1,0:T(8,128)(2,1)} %get-tuple-element.251), kind=kOutput, calls=%fused_computation.2.clone.1 | convolution fusion | flops 12884901888 | bytes 35652096 | tf_op jit(solution)/shard_map/while/body/eval_jaxpr/kit,jt->kij/dot_general | solution.py:23
  458.5 2.9 bitcast_dynamic-update-slice_fusion.18
  461.3 2.9 bitcast_dynamic-update-slice_fusion.19
  464.2 2.9 bitcast_dynamic-update-slice_fusion.20
  481.3 21.1 %bitcast_dynamic-update-slice_fusion.26 = f32[8,8,256,512]{3,2,1,0:T(8,128)} fusion(f32[8,8,256,512]{3,2,1,0:T(8,128)} %get-tuple-element.222, s32[]{:T(128)} %get-tuple-element.221, bf16[8,256,6144]{2,1,0:T(8,128)(2,1)} %bitcast_dynamic-update-slice_fusion.25, bf16[512,6144]{1,0:T(8,128)(2,1)} %get-tuple-element.251), kind=kOutput, calls=%fused_computation.2.clone.1 | convolution fusion | flops 12884901888 | bytes 35652096 | tf_op jit(solution)/shard_map/while/body/eval_jaxpr/kit,jt->kij/dot_general | solution.py:23
  503.7 2.9 bitcast_dynamic-update-slice_fusion.18
  506.5 2.9 bitcast_dynamic-update-slice_fusion.19
  509.4 2.9 bitcast_dynamic-update-slice_fusion.20
  526.4 21.1 %bitcast_dynamic-update-slice_fusion.26 = f32[8,8,256,512]{3,2,1,0:T(8,128)} fusion(f32[8,8,256,512]{3,2,1,0:T(8,128)} %get-tuple-element.222, s32[]{:T(128)} %get-tuple-element.221, bf16[8,256,6144]{2,1,0:T(8,128)(2,1)} %bitcast_dynamic-update-slice_fusion.25, bf16[512,6144]{1,0:T(8,128)(2,1)} %get-tuple-element.251), kind=kOutput, calls=%fused_computation.2.clone.1 | convolution fusion | flops 12884901888 | bytes 35652096 | tf_op jit(solution)/shard_map/while/body/eval_jaxpr/kit,jt->kij/dot_general | solution.py:23
  547.5 23.9 %broadcast_multiply_fusion = f32[8,8,256,512]{3,2,1,0:T(8,128)} fusion(f32[8,8,256,512]{3,2,1,0:T(8,128)} %get-tuple-element.140), kind=kLoop, calls=%fused_computation.11 | loop fusion | flops 8388608 | bytes 67108864 | tf_op jit(solution)/shard_map/mul | solution.py:56
  571.4 48.4 %mul.39 = f32[64,2,128,1,512]{4,3,2,1,0:T(1,128)} reshape(f32[8,8,256,512]{3,2,1,0:T(8,128)} %broadcast_multiply_fusion) | data formatting | bytes 67108864 | tf_op jit(solution)/shard_map/mul | solution.py:56
  (51 shorter events, 107.4 us)
Async XLA Ops:
  6.5 42.1 %all-gather.3.cloned.1.call-start = ((), (), s32[]{:S(2)}) async-start(), calls=%async_computation.1 | async-start | bytes 1966080 | tf_op jit(solution)/shard_map/all_gather | solution.py:41
  53.3 75.9 %all-to-all-start = ((bf16[4,1,512,1536]{3,2,1,0:T(8,128)(2,1)}), bf16[4,1,512,1536]{3,2,1,0:T(8,128)(2,1)}, u32[]{:S(2)}, u32[]{:S(2)}) async-start(bf16[4,1,512,1536]{3,2,1,0:T(8,128)(2,1)} %stack.88), calls=%async_computation | async-start | bytes 12582912 | tf_op jit(solution)/shard_map/all_to_all | solution.py:43
  58.5 125.5 %all-gather.5.cloned.1.call-start = ((), (), s32[]{:S(2)}) async-start(), calls=%async_computation.2 | async-start | bytes 4718592 | tf_op jit(solution)/shard_map/all_gather | solution.py:30
Sparse Core Ops, SparseCore 0:
  8.9 39.7 all-gather.2
  141.1 42.8 all-gather.4
